TPU v7x, 128 devices: a whole 4x4x4 slice. The times are simulated.
128 devices in a mesh: grp: 32 (over y, x, core), col: 4 (over z).
Axes of the slice: x: 4, y: 4, z: 4, core: 2. Of those that a mesh axis runs over, the one named last changes fastest.
Arguments:
- old_tables: bfloat16 [128, 128, 32768], P(('grp', 'col')), may hold values from -3 to 3
- table_rows: int32 [128], replicated, may hold values from 4096 to 32768, as said below
- old_plan: int32 [128], replicated, may hold values from 0 to 127, each once
- new_plan: int32 [128], replicated, may hold values from 0 to 127, each once
- ids: int32 [1024, 128, 16], P(('grp', 'col')), may hold values from 0 to 32767, as said below
- bag_len: int32 [1024, 128], P(('grp', 'col')), may hold values from 1 to 16
Outputs:
- new_tables: bfloat16 [128, 128, 32768], P('grp', 'col')
- pooled: float32 [1024, 128, 128], P(('grp', 'col'))
Inputs may be any that keep to these rules, and one draw needn't show every extreme that they name: table_rows[t] is a multiple of 4096, and some table has exactly 32768 rows. `ids`: every id of table t lies below table_rows[t].
All inputs are finite; a program needn't handle non-finite values.
Results may differ from a plain program's by a relative error of at most 0.001.
Values may be sent and summed in bfloat16 or wider, within the bound.
A program may use at most 128 MiB of HBM per device.

v0:
```python
import jax
import jax.numpy as jnp
from jax import lax
from jax.sharding import PartitionSpec as P


def invert(permutation):
    entries = permutation.shape[0]
    across = lax.broadcasted_iota(jnp.int32, (entries, entries), 1)
    down = lax.broadcasted_iota(jnp.int32, (entries, entries), 0)
    return jnp.sum(jnp.where(permutation[None, :] == down, across, 0), axis=1)


def pool_rows(table_cols, marked):
    columns = table_cols.shape[0]
    safe_ids = jnp.maximum(marked, 0).reshape(-1)
    weights = (marked >= 0).astype(jnp.float32)
    picked = (
        jnp.take(table_cols, safe_ids, axis=1)
        .reshape(columns, marked.shape[0], marked.shape[1])
        .astype(jnp.float32)
    )
    return jnp.sum(picked * weights[None, :, :], axis=2)


def reorder_blocks(spread, source_rows):
    count = spread.shape[0]
    across = lax.broadcasted_iota(jnp.int32, (count, count), 1)
    selector = (source_rows[:, None] == across).astype(spread.dtype)
    flat = spread.reshape(count, -1)
    picked = jnp.dot(selector, flat, preferred_element_type=jnp.float32).astype(spread.dtype)
    return picked.reshape(spread.shape)


def body(old_tables, table_rows, old_plan, new_plan, ids, bag_len):
    group_count = lax.axis_size("grp")
    col_count = lax.axis_size("col")
    device_count = group_count * col_count
    full_width = old_tables.shape[1]
    table_len = old_tables.shape[2]
    row_block = table_len // device_count
    narrow = full_width // col_count
    per_group = new_plan.shape[0] // group_count
    bag_size = ids.shape[2]
    own_slot = lax.axis_index("grp") * col_count + lax.axis_index("col")
    own_table = old_plan[own_slot]
    row_limit = table_rows[own_table]
    row_iota = lax.broadcasted_iota(jnp.int32, (1, table_len), 1)
    owned_table = old_tables[0] * (row_iota < row_limit).astype(old_tables.dtype)
    spread = lax.all_to_all(
        owned_table.reshape(full_width, device_count, row_block),
        ("grp", "col"),
        split_axis=1,
        concat_axis=0,
        tiled=True,
    )
    spread = spread.reshape(device_count * col_count, narrow, row_block)
    old_inverse = invert(old_plan)
    source_slot = old_inverse[new_plan].reshape(group_count, 1, per_group)
    source_rows = (
        source_slot * col_count + lax.broadcasted_iota(jnp.int32, (1, col_count, 1), 1)
    ).reshape(-1)
    blocks = reorder_blocks(spread, source_rows)
    direct = lax.all_to_all(
        blocks.reshape(device_count, per_group, narrow, row_block),
        ("grp", "col"),
        split_axis=0,
        concat_axis=3,
        tiled=True,
    )
    new_local = direct.reshape(per_group, narrow, table_len)
    bag_iota = lax.broadcasted_iota(jnp.int32, (1, 1, bag_size), 2)
    marked = jnp.where(bag_iota < bag_len[:, :, None], ids, -1)
    by_slot = jnp.take(marked, old_plan, axis=1)
    own_ids = lax.all_to_all(
        by_slot, ("grp", "col"), split_axis=1, concat_axis=0, tiled=True
    ).reshape(-1, bag_size)
    partial_value = pool_rows(owned_table, own_ids)
    returned = lax.all_to_all(
        partial_value.reshape(1, full_width, -1),
        ("grp", "col"),
        split_axis=2,
        concat_axis=0,
        tiled=True,
    )
    by_table = jnp.take(returned, old_inverse, axis=0)
    pooled = jnp.transpose(by_table, (2, 0, 1))
    return (new_local, pooled)


def solution(mesh):
    return jax.shard_map(
        body,
        mesh=mesh,
        in_specs=(
            P(("grp", "col"), None, None),
            P(),
            P(),
            P(),
            P(("grp", "col"), None, None),
            P(("grp", "col"), None),
        ),
        out_specs=(P("grp", "col", None), P(("grp", "col"), None, None)),
        check_vma=False,
    )
```

profile of v0, /device:TPU:4, one launch (start us, length us, event | category | flops | bytes accessed | tf_op | source)
XLA Modules:
  0.0 348.2 jit_solution(16318055457653607077)
XLA Ops:
  0.6 0.7 compare_select_fusion.1
  1.3 0.7 compare_and_fusion
  2.0 1.1 copy.25
  3.0 0.8 copy.24
  3.8 0.2 fusion.1
  4.0 0.8 gather_fusion.1
  4.8 0.2 fusion.5
  5.0 0.9 reshape.168
  5.9 10.5 %all-to-all-start.2 = ((s32[128,1,128]{2,1,0:T(1,128)}), s32[128,1,128]{2,1,0:T(1,128)S(1)}, u32[]{:S(2)}, u32[]{:S(2)}) async-start(s32[128,1,128]{2,1,0:T(1,128)} %reshape.168), calls=%async_computation.2 | async-start | bytes 131072 | tf_op jit(solution)/shard_map/all_to_all | solution.py:75
  16.4 1.2 dynamic_slice.6
  18.9 0.8 select_reduce_fusion
  20.4 1.2 dynamic_slice.7
  21.6 0.7 fusion.3
  22.3 0.7 fusion.2
  22.9 0.0 copy-start
  23.0 9.3 %copy.28 = bf16[16,8,128,256]{3,2,1,0:T(8,128)(2,1)} copy(bf16[16,8,128,256]{3,1,2,0:T(8,128)(2,1)} %bitcast.69) | data formatting | bytes 16777216
  32.2 0.0 copy-done
  32.2 1.4 gather_fusion
  33.7 0.1 mul.40
  33.8 15.8 %copy_multiply_fusion = bf16[128,128,256]{2,0,1:T(8,128)(2,1)} fusion(bf16[128,128,256]{2,1,0:T(8,128)(2,1)} %bitcast.71, bf16[128,256]{1,0:T(8,128)(2,1)S(1)} %fusion.2), kind=kLoop, calls=%fused_computation.6 | loop fusion | flops 4194304 | bytes 16842752 | tf_op jit(solution)/shard_map/mul | solution.py:49
  49.6 11.9 %copy.26 = bf16[1,128,32768]{1,2,0:T(8,128)(2,1)} copy(bf16[1,128,32768]{2,1,0:T(8,128)(2,1)} %param.6) | data formatting | bytes 16777216 | tf_op args[0]
  61.5 0.1 add.73
  61.6 0.0 all-to-all-done.2
  61.6 10.2 %all-to-all-start = ((bf16[128,128,256]{2,0,1:T(8,128)(2,1)}), bf16[128,128,256]{2,0,1:T(8,128)(2,1)}, u32[]{:S(2)}, u32[]{:S(2)}) async-start(bf16[128,128,256]{2,0,1:T(8,128)(2,1)} %copy_multiply_fusion), calls=%async_computation | async-start | bytes 16777216 | tf_op jit(solution)/shard_map/all_to_all | solution.py:50
  71.9 8.6 %bitcast_multiply_fusion = bf16[128,32768]{0,1:T(8,128)(2,1)} fusion(bf16[1,128,32768]{1,2,0:T(8,128)(2,1)} %copy.26, bf16[32768]{0:T(1024)(128)(2,1)S(1)} %fusion.3), kind=kLoop, calls=%fused_computation.5 | loop fusion | flops 4194304 | bytes 16842752 | tf_op jit(solution)/shard_map/mul | solution.py:49
  80.4 0.5 broadcast.144
  80.9 0.8 reduce
  81.7 0.2 reshape.169
  82.0 0.2 reshape.151
  82.2 59.6 %gather_fusion.2 = bf16[16384,128]{1,0:T(8,128)(2,1)} fusion(bf16[128,32768]{0,1:T(8,128)(2,1)} %bitcast_multiply_fusion, s32[16384]{0:T(1024)S(1)} %broadcast_clamp_fusion), kind=kCustom, calls=%fused_computation.2 | custom fusion | bytes 8454144 | tf_op jit(solution)/shard_map/jit(_take)/gather | solution.py:19
  141.8 0.1 compare_bitcast_fusion
  141.9 8.1 %multiply_reduce_fusion = f32[128,1024]{0,1:T(8,128)} fusion(f32[1024,16]{1,0:T(8,128)S(1)} %get-tuple-element.9, pred[1024,16]{1,0:T(8,128)(4,1)S(1)} %get-tuple-element.8, bf16[16384,128]{1,0:T(8,128)(2,1)} %gather_fusion.2), kind=kLoop, calls=%fused_computation.7 | loop fusion | flops 8257536 | bytes 4800512 | tf_op jit(solution)/shard_map/reduce_sum | solution.py:23
  150.0 20.3 %all-to-all-done = bf16[128,128,256]{2,0,1:T(8,128)(2,1)} async-done(((bf16[128,128,256]{2,0,1:T(8,128)(2,1)}), bf16[128,128,256]{2,0,1:T(8,128)(2,1)}, u32[]{:S(2)}, u32[]{:S(2)}) %all-to-all-start) | async-done | bytes 8388640 | tf_op jit(solution)/shard_map/all_to_all | solution.py:50
  170.3 11.1 %all-to-all-start.3 = ((f32[1,128,1024]{1,0,2:T(1,128)}), f32[1,128,1024]{1,0,2:T(1,128)S(1)}, u32[]{:S(2)}, u32[]{:S(2)}) async-start(f32[1,128,1024]{1,0,2:T(1,128)} %bitcast.18), calls=%async_computation.3 | async-start | bytes 1048576 | tf_op jit(solution)/shard_map/all_to_all | solution.py:79
  181.4 13.4 %reshape_reshape.6 = bf16[512,8192]{1,0:T(8,128)(2,1)} reshape(bf16[128,128,1,256]{3,1,0,2:T(8,128)(2,1)} %bitcast.3) | data formatting | bytes 16777216 | tf_op jit(solution)/shard_map/reshape;reshape | solution.py:30
  194.8 10.1 %convolution_convert_fusion = bf16[512,8192]{1,0:T(8,128)(2,1)} fusion(bf16[512,8192]{1,0:T(8,128)(2,1)} %reshape_reshape.6, s32[512]{0:T(512)S(1)} %add.73), kind=kOutput, calls=%fused_computation.4 | convolution fusion | flops 4299423744 | bytes 16779264 | tf_op jit(solution)/shard_map/dot_general | solution.py:31
  205.0 9.7 %copy.29 = bf16[64,8,32,256]{3,2,1,0:T(8,128)(2,1)} copy(bf16[64,8,32,256]{3,1,2,0:T(8,128)(2,1)} %bitcast.72) | data formatting | bytes 16777216
  214.7 0.0 all-to-all-done.3
  214.7 10.2 %all-to-all-start.1 = ((bf16[128,4,32,256]{3,2,1,0:T(8,128)(2,1)}), bf16[128,4,32,256]{3,2,1,0:T(8,128)(2,1)}, u32[]{:S(2)}, u32[]{:S(2)}) async-start(bf16[128,4,32,256]{3,2,1,0:T(8,128)(2,1)} %bitcast.70), calls=%async_computation.1 | async-start | bytes 16777216 | tf_op jit(solution)/shard_map/all_to_all | solution.py:64
  225.0 0.8 gather_fusion.3
  225.7 0.2 select_bitcast_fusion.1
  225.9 0.9 copy.27
  226.8 96.5 %all-to-all-done.1 = bf16[128,4,32,256]{3,2,1,0:T(8,128)(2,1)} async-done(((bf16[128,4,32,256]{3,2,1,0:T(8,128)(2,1)}), bf16[128,4,32,256]{3,2,1,0:T(8,128)(2,1)}, u32[]{:S(2)}, u32[]{:S(2)}) %all-to-all-start.1) | async-done | bytes 8388640 | tf_op jit(solution)/shard_map/all_to_all | solution.py:64
  323.3 11.5 %copy.23 = bf16[1,4,32,128,256]{4,3,2,1,0:T(8,128)(2,1)} copy(bf16[1,4,32,128,256]{4,2,1,3,0:T(8,128)(2,1)} %bitcast.5) | data formatting | bytes 16777216 | tf_op jit(solution)/shard_map/all_to_all | solution.py:64
  334.8 13.4 %reshape.129 = bf16[4,32,32768]{2,1,0:T(8,128)(2,1)} reshape(bf16[1,4,32,128,256]{4,3,2,1,0:T(8,128)(2,1)} %copy.23) | data formatting | bytes 16777216 | tf_op jit(solution)/shard_map/reshape | solution.py:71
  (10 shorter events, 0.1 us)
Async XLA Ops:
  5.9 55.7 %all-to-all-start.2 = ((s32[128,1,128]{2,1,0:T(1,128)}), s32[128,1,128]{2,1,0:T(1,128)S(1)}, u32[]{:S(2)}, u32[]{:S(2)}) async-start(s32[128,1,128]{2,1,0:T(1,128)} %reshape.168), calls=%async_computation.2 | async-start | bytes 131072 | tf_op jit(solution)/shard_map/all_to_all | solution.py:75
  22.9 9.3 %copy-start = (s32[128]{0:T(128)S(1)}, s32[128]{0:T(128)}, u32[]{:S(2)}) copy-start(s32[128]{0:T(128)} %param.9) | copy-start | bytes 1540
  61.6 108.7 %all-to-all-start = ((bf16[128,128,256]{2,0,1:T(8,128)(2,1)}), bf16[128,128,256]{2,0,1:T(8,128)(2,1)}, u32[]{:S(2)}, u32[]{:S(2)}) async-start(bf16[128,128,256]{2,0,1:T(8,128)(2,1)} %copy_multiply_fusion), calls=%async_computation | async-start | bytes 16777216 | tf_op jit(solution)/shard_map/all_to_all | solution.py:50
  170.3 44.4 %all-to-all-start.3 = ((f32[1,128,1024]{1,0,2:T(1,128)}), f32[1,128,1024]{1,0,2:T(1,128)S(1)}, u32[]{:S(2)}, u32[]{:S(2)}) async-start(f32[1,128,1024]{1,0,2:T(1,128)} %bitcast.18), calls=%async_computation.3 | async-start | bytes 1048576 | tf_op jit(solution)/shard_map/all_to_all | solution.py:79
  214.7 108.7 %all-to-all-start.1 = ((bf16[128,4,32,256]{3,2,1,0:T(8,128)(2,1)}), bf16[128,4,32,256]{3,2,1,0:T(8,128)(2,1)}, u32[]{:S(2)}, u32[]{:S(2)}) async-start(bf16[128,4,32,256]{3,2,1,0:T(8,128)(2,1)} %bitcast.70), calls=%async_computation.1 | async-start | bytes 16777216 | tf_op jit(solution)/shard_map/all_to_all | solution.py:64
where the time goes:
time: 355 us; the launch traced here: 348 us
  local copies, waits for them, and re-layouts  139 us (39%)
  waiting for transfers between devices  117 us (33%)
  starting transfers between devices  42.1 us (12%)
  other arithmetic  37.5 us (11%)
  matrix products  10.1 us (3%)
    all_to_all x1, waiting for transfers between devices, body(): lax.all_to_all(blocks.reshape(device_count, per_group, narrow, row_block)...  96.5 us
    gather x1, local copies, waits for them, and re-layouts, pool_rows(): jnp.take(table_cols, safe_ids, axis=1)  59.6 us
    unnamed x10, local copies, waits for them, and re-layouts  34.7 us
    mul x2, other arithmetic, body(): old_tables[0] * (row_iota < row_limit).astype(old_tables.dtype)  24.4 us
    all_to_all x1, waiting for transfers between devices, body(): lax.all_to_all(owned_table.reshape(full_width, device_count, row_block),...  20.3 us
    another operation x1, local copies, waits for them, and re-layouts, reorder_blocks(): flat = spread.reshape(count, -1)  13.4 us
    reshape x1, local copies, waits for them, and re-layouts, body(): new_local = direct.reshape(per_group, narrow, table_len)  13.4 us
    all_to_all x1, local copies, waits for them, and re-layouts, body(): lax.all_to_all(blocks.reshape(device_count, per_group, narrow, row_block)...  11.5 us
  transfers between devices with their start and end apart: 4, of which 2 were waited for; matrix products, arithmetic and copies ran while one was open for 45% of the time, Pallas kernels for 0%

commit v1 on v0

v1 whole, which is shorter than its diff:
```python
import functools

import jax
import jax.numpy as jnp
from jax import lax
from jax.experimental import pallas as pl
from jax.experimental.pallas import tpu as pltpu
from jax.sharding import PartitionSpec as P

MESH = pl.DeviceIdType.MESH
LANES = 128
UNIT = 4096


def invert(permutation):
    entries = permutation.shape[0]
    across = lax.broadcasted_iota(jnp.int32, (entries, entries), 1)
    down = lax.broadcasted_iota(jnp.int32, (entries, entries), 0)
    return jnp.sum(jnp.where(permutation[None, :] == down, across, 0), axis=1)


def pool_rows(table_cols, marked):
    columns = table_cols.shape[0]
    safe_ids = jnp.maximum(marked, 0).reshape(-1)
    weights = (marked >= 0).astype(jnp.float32)
    picked = (
        jnp.take(table_cols, safe_ids, axis=1)
        .reshape(columns, marked.shape[0], marked.shape[1])
        .astype(jnp.float32)
    )
    return jnp.sum(picked * weights[None, :, :], axis=2)


def place(index):
    core = lax.rem(index, 2)
    x = lax.rem(lax.div(index, 2), 4)
    y = lax.rem(lax.div(index, 8), 4)
    z = lax.div(index, 32)
    return y, x, core, z


def peer_of(offset, me):
    dy, dx, dc, dz = place(offset)
    y, x, core, z = me
    ty, tx = lax.rem(y + dy, 4), lax.rem(x + dx, 4)
    tc, tz = lax.rem(core + dc, 2), lax.rem(z + dz, 4)
    return (ty * 4 + tx) * 2 + tc, tz


def exchange_kernel(
    groups, cols, stride, slots_ref, units_ref, table_ref, out_ref,
    blocks, landed, packed, local_sem, send_sem, recv_sem, send2_sem, recv2_sem,
):
    devices = groups * cols
    width = table_ref.shape[1]
    narrow = width // cols
    column_blocks = table_ref.shape[2] // LANES
    units = column_blocks // groups
    grp = lax.axis_index("grp")
    col = lax.axis_index("col")
    own = grp * cols + col
    me = (lax.div(grp, 8), lax.rem(lax.div(grp, 2), 4), lax.rem(grp, 2), col)

    def load(j, carry):
        pltpu.make_async_copy(
            table_ref.at[0, :, pl.ds(pl.multiple_of(j * LANES, LANES), LANES)],
            blocks.at[lax.div(j, groups), lax.rem(j, groups)],
            local_sem,
        ).start()
        return carry

    lax.fori_loop(0, column_blocks, load, 0)
    pltpu.make_async_copy(blocks, blocks, local_sem).wait()

    def send(i, carry):
        offset = lax.rem(i * stride, devices)
        to_grp, to_col = peer_of(offset, me)
        pltpu.make_async_remote_copy(
            src_ref=blocks.at[:, to_grp, pl.ds(pl.multiple_of(to_col * narrow, narrow), narrow), :],
            dst_ref=landed.at[own],
            send_sem=send_sem,
            recv_sem=recv_sem,
            device_id=(to_grp, to_col),
            device_id_type=MESH,
        ).start()
        return carry

    lax.fori_loop(1, devices, send, 0)
    landed[own] = blocks[:, grp, pl.ds(pl.multiple_of(col * narrow, narrow), narrow), :]
    everyone = landed.at[pl.ds(0, devices - 1)]
    pltpu.make_async_copy(everyone, everyone, recv_sem).wait()

    per_group = packed.shape[1]

    def pack(j, carry):
        slot = slots_ref[j]
        count = units_ref[j]
        block = landed[slot]
        unit = lax.broadcasted_iota(jnp.int32, block.shape, 0)
        packed[lax.div(j, per_group), lax.rem(j, per_group)] = jnp.where(
            unit < count, block, jnp.zeros_like(block)
        )
        return carry

    lax.fori_loop(0, groups * per_group, pack, 0)

    def send2(i, carry):
        offset = lax.rem(i * 5, groups)
        to_grp, _ = peer_of(offset, me)
        pltpu.make_async_remote_copy(
            src_ref=packed.at[to_grp],
            dst_ref=out_ref.at[grp],
            send_sem=send2_sem,
            recv_sem=recv2_sem,
            device_id=(to_grp, col),
            device_id_type=MESH,
        ).start()
        return carry

    lax.fori_loop(1, groups, send2, 0)
    mine = pltpu.make_async_copy(packed.at[grp], out_ref.at[grp], local_sem)
    mine.start()
    mine.wait()
    pltpu.make_async_copy(everyone, everyone, send_sem).wait()
    others = packed.at[pl.ds(0, groups - 1)]
    pltpu.make_async_copy(others, others, send2_sem).wait()
    pltpu.make_async_copy(out_ref.at[pl.ds(0, groups - 1)], out_ref.at[pl.ds(0, groups - 1)], recv2_sem).wait()


def exchange(slots, counts, old_tables, groups, cols, stride=37):
    _, width, table_len = old_tables.shape
    devices = groups * cols
    narrow = width // cols
    per_group = slots.shape[0] // groups
    column_blocks = table_len // LANES
    units = column_blocks // groups
    dtype = old_tables.dtype
    return pl.pallas_call(
        functools.partial(exchange_kernel, groups, cols, stride),
        out_shape=jax.ShapeDtypeStruct((groups, per_group, units, narrow, LANES), dtype),
        in_specs=[
            pl.BlockSpec(memory_space=pltpu.SMEM),
            pl.BlockSpec(memory_space=pltpu.SMEM),
            pl.BlockSpec(memory_space=pl.ANY),
        ],
        out_specs=pl.BlockSpec(memory_space=pl.ANY),
        scratch_shapes=[
            pltpu.VMEM((units, groups, width, LANES), dtype),
            pltpu.VMEM((devices, units, narrow, LANES), dtype),
            pltpu.VMEM((groups, per_group, units, narrow, LANES), dtype),
            pltpu.SemaphoreType.DMA,
            pltpu.SemaphoreType.DMA,
            pltpu.SemaphoreType.DMA,
            pltpu.SemaphoreType.DMA,
            pltpu.SemaphoreType.DMA,
        ],
        compiler_params=pltpu.CompilerParams(
            has_side_effects=True, vmem_limit_bytes=60 * 1024 * 1024
        ),
        name="exchange",
    )(slots, counts, old_tables)


def unpack_kernel(in_ref, out_ref):
    groups, _, units = in_ref.shape[:3]
    for k in range(units):
        for p in range(groups):
            start = (k * groups + p) * LANES
            out_ref[0, :, start : start + LANES] = in_ref[p, 0, k]


def unpack(received, step=2):
    groups, per_group, units, narrow, lanes = received.shape
    return pl.pallas_call(
        unpack_kernel,
        out_shape=jax.ShapeDtypeStruct((per_group, narrow, units * groups * lanes), received.dtype),
        grid=(per_group, units // step),
        in_specs=[pl.BlockSpec((groups, 1, step, narrow, lanes), lambda q, k: (0, q, k, 0, 0))],
        out_specs=pl.BlockSpec((1, narrow, step * groups * lanes), lambda q, k: (q, 0, k)),
        name="unpack",
    )(received)


def body(old_tables, table_rows, old_plan, new_plan, ids, bag_len):
    group_count = lax.axis_size("grp")
    col_count = lax.axis_size("col")
    full_width = old_tables.shape[1]
    bag_size = ids.shape[2]
    old_inverse = invert(old_plan)
    slots = old_inverse[new_plan]
    counts = table_rows[new_plan] // UNIT
    received = exchange(slots, counts, old_tables, group_count, col_count)
    new_local = unpack(received)

    bag_iota = lax.broadcasted_iota(jnp.int32, (1, 1, bag_size), 2)
    marked = jnp.where(bag_iota < bag_len[:, :, None], ids, -1)
    by_slot = jnp.take(marked, old_plan, axis=1)
    own_ids = lax.all_to_all(
        by_slot, ("grp", "col"), split_axis=1, concat_axis=0, tiled=True
    ).reshape(-1, bag_size)
    partial_value = pool_rows(old_tables[0], own_ids)
    returned = lax.all_to_all(
        partial_value.reshape(1, full_width, -1),
        ("grp", "col"),
        split_axis=2,
        concat_axis=0,
        tiled=True,
    )
    by_table = jnp.take(returned, old_inverse, axis=0)
    pooled = jnp.transpose(by_table, (2, 0, 1))
    return (new_local, pooled)


def solution(mesh):
    return jax.shard_map(
        body,
        mesh=mesh,
        in_specs=(
            P(("grp", "col"), None, None),
            P(),
            P(),
            P(),
            P(("grp", "col"), None, None),
            P(("grp", "col"), None),
        ),
        out_specs=(P("grp", "col", None), P(("grp", "col"), None, None)),
        check_vma=False,
    )
```

time: 355 us -> 379 us (1.068)
  Pallas kernels: 0 us -> 242 us
  waiting for transfers between devices: 117 us -> 12.3 us
  local copies, waits for them, and re-layouts: 139 us -> 80.4 us
  other arithmetic: 37.5 us -> 11.7 us
  starting transfers between devices: 42.1 us -> 28.4 us
  matrix products: 10.1 us -> 0 us
    pallas_call x0 -> x2, Pallas kernels: none -> 242 us  [the longest x1 229 us: exchange(): pl.pallas_call(functools.partial(exchange_kernel, groups, cols, stride),...]
    all_to_all x2 -> x0, waiting for transfers between devices: 117 us -> none  [the longest x1 96.5 us: body(): lax.all_to_all(blocks.reshape(device_count, per_group, narrow, row_block)...]
    mul x3 -> x0, other arithmetic: 24.4 us -> none  [the longest x2 24.4 us: body(): old_tables[0] * (row_iota < row_limit).astype(old_tables.dtype)]
    all_to_all x2 -> x0, starting transfers between devices: 20.5 us -> none  [the longest x1 10.2 us: body(): lax.all_to_all(owned_table.reshape(full_width, device_count, row_block),...]
    unnamed x10 -> x12, local copies, waits for them, and re-layouts: 34.7 us -> 15.7 us
    another operation x1 -> x0, local copies, waits for them, and re-layouts: 13.4 us -> none  [reorder_blocks(): flat = spread.reshape(count, -1)]
    reshape x1 -> x0, local copies, waits for them, and re-layouts: 13.4 us -> none  [body(): new_local = direct.reshape(per_group, narrow, table_len)]
    all_to_all x1, waiting for transfers between devices: 0.01 us -> 12.3 us  [body(): lax.all_to_all(partial_value.reshape(1, full_width, -1), ('grp', 'col'),...]
  transfers between devices with their start and end apart: 4 -> 2, of which waited for: 2 -> 1; matrix products, arithmetic and copies ran while one was open for 45% -> 4% of each run, Pallas kernels for 0% -> 64%
where the time goes in v1:
time: 379 us; the launch traced here: 375 us
  Pallas kernels  242 us (64%)
  local copies, waits for them, and re-layouts  80.4 us (21%)
  starting transfers between devices  28.4 us (7%)
  waiting for transfers between devices  12.3 us (3%)
  other arithmetic  11.7 us (3%)
    pallas_call x1, Pallas kernels, exchange(): pl.pallas_call(functools.partial(exchange_kernel, groups, cols, stride),...  229 us
    gather x1, local copies, waits for them, and re-layouts, pool_rows(): jnp.take(table_cols, safe_ids, axis=1)  59.5 us
    all_to_all x1, starting transfers between devices, body(): lax.all_to_all(partial_value.reshape(1, full_width, -1), ('grp', 'col'),...  17.9 us
    unnamed x12, local copies, waits for them, and re-layouts  15.7 us
    pallas_call x1, Pallas kernels, unpack(): pl.pallas_call(unpack_kernel, out_shape=jax.ShapeDtypeStruct((per_group,...  12.4 us
    all_to_all x1, waiting for transfers between devices, body(): lax.all_to_all(partial_value.reshape(1, full_width, -1), ('grp', 'col'),...  12.3 us
    all_to_all x1, starting transfers between devices, body(): lax.all_to_all(by_slot, ('grp', 'col'), split_axis=1, concat_axis=0, tile...  10.5 us
    reduce_sum x1, other arithmetic, pool_rows(): return jnp.sum(picked * weights[None, :, :], axis=2)  8.1 us
  transfers between devices with their start and end apart: 2, of which 1 were waited for; matrix products, arithmetic and copies ran while one was open for 4% of the time, Pallas kernels for 64%

profile of v1, /device:TPU:4, one launch (start us, length us, event | category | flops | bytes accessed | tf_op | source)
XLA Modules:
  0.0 375.5 jit_solution(15646072638636675682)
XLA Ops:
  0.6 0.0 copy-start
  0.6 0.7 compare_select_fusion.1
  1.3 0.7 compare_and_fusion
  2.0 1.1 copy.18
  3.1 0.8 copy.17
  3.8 0.2 fusion
  4.1 0.8 gather_fusion.2
  4.8 0.2 fusion.2
  5.0 0.9 reshape.132
  5.9 10.5 %all-to-all-start = ((s32[128,1,128]{2,1,0:T(1,128)}), s32[128,1,128]{2,1,0:T(1,128)S(1)}, u32[]{:S(2)}, u32[]{:S(2)}) async-start(s32[128,1,128]{2,1,0:T(1,128)} %reshape.132), calls=%async_computation | async-start | bytes 131072 | tf_op jit(solution)/shard_map/all_to_all | solution.py:198
  16.4 0.0 copy-start.1
  16.4 0.0 copy-start.2
  16.4 11.9 %copy.19 = bf16[1,128,32768]{1,2,0:T(8,128)(2,1)} copy(bf16[1,128,32768]{2,1,0:T(8,128)(2,1)} %table_ref.1) | data formatting | bytes 16777216 | tf_op args[0]
  28.4 0.0 copy-done.1
  28.4 0.0 copy-done
  28.4 1.2 gather_fusion.1
  29.6 0.5 and_select_fusion.units_ref
  30.1 0.0 copy-done.2
  30.1 0.1 select_reduce_fusion
  30.2 1.7 gather_fusion
  32.0 229.5 %exchange.1.in_ref = bf16[32,4,8,32,128]{4,3,2,1,0:T(8,128)(2,1)} custom-call(s32[128]{0:T(128)} %gather_fusion, s32[128]{0:T(128)} %and_select_fusion.units_ref, bf16[1,128,32768]{2,1,0:T(8,128)(2,1)} %table_ref.1), custom_call_target="tpu_custom_call" | custom-call | tf_op jit(solution)/shard_map/exchange/pallas_call | solution.py:138
  261.4 12.4 %unpack.1 = bf16[4,32,32768]{2,1,0:T(8,128)(2,1)} custom-call(bf16[32,4,8,32,128]{4,3,2,1,0:T(8,128)(2,1)} %exchange.1.in_ref), custom_call_target="tpu_custom_call" | custom-call | tf_op jit(solution)/shard_map/unpack/pallas_call | solution.py:174
  273.8 0.0 all-to-all-done
  273.8 0.5 broadcast.158
  274.3 0.8 reduce
  275.2 0.2 reshape.133
  275.3 0.1 compare_bitcast_fusion
  275.5 0.2 reshape.114
  275.8 59.5 %gather_fusion.3 = bf16[16384,128]{1,0:T(8,128)(2,1)} fusion(bf16[128,32768]{0,1:T(8,128)(2,1)} %bitcast.46, s32[16384]{0:T(1024)S(1)} %broadcast_clamp_fusion), kind=kCustom, calls=%fused_computation.3 | custom fusion | bytes 8454144 | tf_op jit(solution)/shard_map/jit(_take)/gather | solution.py:27
  335.3 8.1 %multiply_reduce_fusion = f32[128,1024]{0,1:T(8,128)} fusion(f32[1024,16]{1,0:T(8,128)S(1)} %get-tuple-element.9, pred[1024,16]{1,0:T(8,128)(4,1)S(1)} %get-tuple-element.8, bf16[16384,128]{1,0:T(8,128)(2,1)} %gather_fusion.3), kind=kLoop, calls=%fused_computation.5 | loop fusion | flops 8257536 | bytes 4800512 | tf_op jit(solution)/shard_map/reduce_sum | solution.py:31
  343.4 17.9 %all-to-all-start.1 = ((f32[1,128,1024]{1,0,2:T(1,128)}), f32[1,128,1024]{1,0,2:T(1,128)S(1)}, u32[]{:S(2)}, u32[]{:S(2)}) async-start(f32[1,128,1024]{1,0,2:T(1,128)} %bitcast.12), calls=%async_computation.1 | async-start | bytes 1048576 | tf_op jit(solution)/shard_map/all_to_all | solution.py:202
  361.4 12.3 %all-to-all-done.1 = f32[1,128,1024]{1,0,2:T(1,128)S(1)} async-done(((f32[1,128,1024]{1,0,2:T(1,128)}), f32[1,128,1024]{1,0,2:T(1,128)S(1)}, u32[]{:S(2)}, u32[]{:S(2)}) %all-to-all-start.1) | async-done | bytes 524320 | tf_op jit(solution)/shard_map/all_to_all | solution.py:202
  373.6 0.8 gather_fusion.4
  374.4 0.2 select_bitcast_fusion.1
  374.6 0.9 copy.20
  (8 shorter events, 0.1 us)
Async XLA Ops:
  0.6 27.7 %copy-start = (s32[128]{0:T(128)S(1)}, s32[128]{0:T(128)}, u32[]{:S(2)}) copy-start(s32[128]{0:T(128)} %param.7) | copy-start | bytes 1540
  5.9 267.9 %all-to-all-start = ((s32[128,1,128]{2,1,0:T(1,128)}), s32[128,1,128]{2,1,0:T(1,128)S(1)}, u32[]{:S(2)}, u32[]{:S(2)}) async-start(s32[128,1,128]{2,1,0:T(1,128)} %reshape.132), calls=%async_computation | async-start | bytes 131072 | tf_op jit(solution)/shard_map/all_to_all | solution.py:198
  16.4 12.0 %copy-start.1 = (s32[128]{0:T(128)S(1)}, s32[128]{0:T(128)}, u32[]{:S(2)}) copy-start(s32[128]{0:T(128)} %param.9) | copy-start | bytes 1540
  16.4 13.7 %copy-start.2 = (s32[128]{0:T(128)S(1)}, s32[128]{0:T(128)}, u32[]{:S(2)}) copy-start(s32[128]{0:T(128)} %param.8) | copy-start | bytes 1540
  343.4 30.3 %all-to-all-start.1 = ((f32[1,128,1024]{1,0,2:T(1,128)}), f32[1,128,1024]{1,0,2:T(1,128)S(1)}, u32[]{:S(2)}, u32[]{:S(2)}) async-start(f32[1,128,1024]{1,0,2:T(1,128)} %bitcast.12), calls=%async_computation.1 | async-start | bytes 1048576 | tf_op jit(solution)/shard_map/all_to_all | solution.py:202

commit v2 on v1

--- a/solution.py
+++ b/solution.py
@@ -10,6 +10,7 @@
 MESH = pl.DeviceIdType.MESH
 LANES = 128
 UNIT = 4096
+BAG = 16
 
 
 def invert(permutation):
@@ -17,18 +18,6 @@
     across = lax.broadcasted_iota(jnp.int32, (entries, entries), 1)
     down = lax.broadcasted_iota(jnp.int32, (entries, entries), 0)
     return jnp.sum(jnp.where(permutation[None, :] == down, across, 0), axis=1)
-
-
-def pool_rows(table_cols, marked):
-    columns = table_cols.shape[0]
-    safe_ids = jnp.maximum(marked, 0).reshape(-1)
-    weights = (marked >= 0).astype(jnp.float32)
-    picked = (
-        jnp.take(table_cols, safe_ids, axis=1)
-        .reshape(columns, marked.shape[0], marked.shape[1])
-        .astype(jnp.float32)
-    )
-    return jnp.sum(picked * weights[None, :, :], axis=2)
 
 
 def place(index):
@@ -48,8 +37,10 @@
 
 
 def exchange_kernel(
-    groups, cols, stride, slots_ref, units_ref, table_ref, out_ref,
-    blocks, landed, packed, local_sem, send_sem, recv_sem, send2_sem, recv2_sem,
+    groups, cols, stride, slots_ref, units_ref, ids_ref, table_ref, out_ref, ret_ref,
+    blocks, landed, packed, rows_by_id, ids_in, ids_smem, sums,
+    local_sem, send_sem, recv_sem, send2_sem, recv2_sem,
+    ids_send_sem, ids_recv_sem, sum_send_sem, sum_recv_sem,
 ):
     devices = groups * cols
     width = table_ref.shape[1]
@@ -70,6 +61,21 @@
         return carry
 
     lax.fori_loop(0, column_blocks, load, 0)
+
+    def send_ids(i, carry):
+        to_grp, to_col = peer_of(lax.rem(i * stride, devices), me)
+        pltpu.make_async_remote_copy(
+            src_ref=ids_ref.at[to_grp * cols + to_col],
+            dst_ref=ids_in.at[own],
+            send_sem=ids_send_sem,
+            recv_sem=ids_recv_sem,
+            device_id=(to_grp, to_col),
+            device_id_type=MESH,
+        ).start()
+        return carry
+
+    lax.fori_loop(1, devices, send_ids, 0)
+    ids_in[own] = ids_ref[own]
     pltpu.make_async_copy(blocks, blocks, local_sem).wait()
 
     def send(i, carry):
@@ -87,6 +93,50 @@
 
     lax.fori_loop(1, devices, send, 0)
     landed[own] = blocks[:, grp, pl.ds(pl.multiple_of(col * narrow, narrow), narrow), :]
+
+    table_len = column_blocks * LANES
+
+    def turn(j, carry):
+        block = blocks[lax.div(j, groups), lax.rem(j, groups)].astype(jnp.float32)
+        rows_by_id[pl.ds(pl.multiple_of(j * LANES, LANES), LANES), :] = block.T
+        return carry
+
+    lax.fori_loop(0, column_blocks, turn, 0)
+    rows_by_id[pl.ds(table_len, 8), :] = jnp.zeros((8, width), jnp.float32)
+    others_ids = ids_in.at[pl.ds(0, devices - 1)]
+    pltpu.make_async_copy(others_ids, others_ids, ids_recv_sem).wait()
+    to_smem = pltpu.make_async_copy(ids_in, ids_smem, local_sem)
+    to_smem.start()
+    to_smem.wait()
+    samples = sums.shape[1]
+    bag = LANES // samples
+
+    def pool(d, carry):
+        for b in range(samples):
+            terms = [rows_by_id[pl.ds(ids_smem[d, 0, b * bag + i], 1), :] for i in range(bag)]
+            while len(terms) > 1:
+                terms = [terms[k] + terms[k + 1] for k in range(0, len(terms), 2)]
+            sums[d, b : b + 1, :] = terms[0]
+        return carry
+
+    lax.fori_loop(0, devices, pool, 0)
+
+    def send_sums(i, carry):
+        to_grp, to_col = peer_of(lax.rem(i * stride, devices), me)
+        pltpu.make_async_remote_copy(
+            src_ref=sums.at[to_grp * cols + to_col],
+            dst_ref=ret_ref.at[own],
+            send_sem=sum_send_sem,
+            recv_sem=sum_recv_sem,
+            device_id=(to_grp, to_col),
+            device_id_type=MESH,
+        ).start()
+        return carry
+
+    lax.fori_loop(1, devices, send_sums, 0)
+    own_sums = pltpu.make_async_copy(sums.at[own], ret_ref.at[own], local_sem)
+    own_sums.start()
+    own_sums.wait()
     everyone = landed.at[pl.ds(0, devices - 1)]
     pltpu.make_async_copy(everyone, everyone, recv_sem).wait()
 
@@ -124,10 +174,16 @@
     pltpu.make_async_copy(everyone, everyone, send_sem).wait()
     others = packed.at[pl.ds(0, groups - 1)]
     pltpu.make_async_copy(others, others, send2_sem).wait()
-    pltpu.make_async_copy(out_ref.at[pl.ds(0, groups - 1)], out_ref.at[pl.ds(0, groups - 1)], recv2_sem).wait()
-
-
-def exchange(slots, counts, old_tables, groups, cols, stride=37):
+    others_out = out_ref.at[pl.ds(0, groups - 1)]
+    pltpu.make_async_copy(others_out, others_out, recv2_sem).wait()
+    pltpu.make_async_copy(others_ids, others_ids, ids_send_sem).wait()
+    others_sums = sums.at[pl.ds(0, devices - 1)]
+    pltpu.make_async_copy(others_sums, others_sums, sum_send_sem).wait()
+    others_ret = ret_ref.at[pl.ds(0, devices - 1)]
+    pltpu.make_async_copy(others_ret, others_ret, sum_recv_sem).wait()
+
+
+def exchange(slots, counts, ids, old_tables, groups, cols, stride=37):
     _, width, table_len = old_tables.shape
     devices = groups * cols
     narrow = width // cols
@@ -135,30 +191,35 @@
     column_blocks = table_len // LANES
     units = column_blocks // groups
     dtype = old_tables.dtype
+    samples = LANES // BAG
     return pl.pallas_call(
         functools.partial(exchange_kernel, groups, cols, stride),
-        out_shape=jax.ShapeDtypeStruct((groups, per_group, units, narrow, LANES), dtype),
+        out_shape=(
+            jax.ShapeDtypeStruct((groups, per_group, units, narrow, LANES), dtype),
+            jax.ShapeDtypeStruct((devices, samples, width), jnp.float32),
+        ),
         in_specs=[
             pl.BlockSpec(memory_space=pltpu.SMEM),
             pl.BlockSpec(memory_space=pltpu.SMEM),
+            pl.BlockSpec(memory_space=pltpu.VMEM),
             pl.BlockSpec(memory_space=pl.ANY),
         ],
-        out_specs=pl.BlockSpec(memory_space=pl.ANY),
+        out_specs=(pl.BlockSpec(memory_space=pl.ANY), pl.BlockSpec(memory_space=pl.ANY)),
         scratch_shapes=[
             pltpu.VMEM((units, groups, width, LANES), dtype),
             pltpu.VMEM((devices, units, narrow, LANES), dtype),
             pltpu.VMEM((groups, per_group, units, narrow, LANES), dtype),
-            pltpu.SemaphoreType.DMA,
-            pltpu.SemaphoreType.DMA,
-            pltpu.SemaphoreType.DMA,
-            pltpu.SemaphoreType.DMA,
-            pltpu.SemaphoreType.DMA,
-        ],
+            pltpu.VMEM((table_len + 8, width), jnp.float32),
+            pltpu.VMEM((devices, 1, LANES), jnp.int32),
+            pltpu.SMEM((devices, 1, LANES), jnp.int32),
+            pltpu.VMEM((devices, samples, width), jnp.float32),
+        ]
+        + [pltpu.SemaphoreType.DMA] * 9,
         compiler_params=pltpu.CompilerParams(
             has_side_effects=True, vmem_limit_bytes=60 * 1024 * 1024
         ),
         name="exchange",
-    )(slots, counts, old_tables)
+    )(slots, counts, ids, old_tables)
 
 
 def unpack_kernel(in_ref, out_ref):
@@ -184,30 +245,18 @@
 def body(old_tables, table_rows, old_plan, new_plan, ids, bag_len):
     group_count = lax.axis_size("grp")
     col_count = lax.axis_size("col")
-    full_width = old_tables.shape[1]
     bag_size = ids.shape[2]
     old_inverse = invert(old_plan)
     slots = old_inverse[new_plan]
     counts = table_rows[new_plan] // UNIT
-    received = exchange(slots, counts, old_tables, group_count, col_count)
+    bag_iota = lax.broadcasted_iota(jnp.int32, (1, 1, bag_size), 2)
+    marked = jnp.where(bag_iota < bag_len[:, :, None], ids, old_tables.shape[2])
+    by_slot = jnp.take(marked, old_plan, axis=1)
+    own_ids = jnp.transpose(by_slot, (1, 0, 2)).reshape(-1, 1, LANES)
+    received, returned = exchange(slots, counts, own_ids, old_tables, group_count, col_count)
     new_local = unpack(received)
-
-    bag_iota = lax.broadcasted_iota(jnp.int32, (1, 1, bag_size), 2)
-    marked = jnp.where(bag_iota < bag_len[:, :, None], ids, -1)
-    by_slot = jnp.take(marked, old_plan, axis=1)
-    own_ids = lax.all_to_all(
-        by_slot, ("grp", "col"), split_axis=1, concat_axis=0, tiled=True
-    ).reshape(-1, bag_size)
-    partial_value = pool_rows(old_tables[0], own_ids)
-    returned = lax.all_to_all(
-        partial_value.reshape(1, full_width, -1),
-        ("grp", "col"),
-        split_axis=2,
-        concat_axis=0,
-        tiled=True,
-    )
     by_table = jnp.take(returned, old_inverse, axis=0)
-    pooled = jnp.transpose(by_table, (2, 0, 1))
+    pooled = jnp.transpose(by_table, (1, 0, 2))
     return (new_local, pooled)
 
 

time: 379 us -> 281 us (0.74)
  local copies, waits for them, and re-layouts: 80.4 us -> 9.09 us
  starting transfers between devices: 28.4 us -> 0 us
  Pallas kernels: 242 us -> 267 us
  waiting for transfers between devices: 12.3 us -> 0 us
  other arithmetic: 11.7 us -> 3.94 us
    gather x1 -> x0, local copies, waits for them, and re-layouts: 59.5 us -> none  [pool_rows(): jnp.take(table_cols, safe_ids, axis=1)]
    all_to_all x2 -> x0, starting transfers between devices: 28.4 us -> none  [the longest x1 17.9 us: body(): lax.all_to_all(partial_value.reshape(1, full_width, -1), ('grp', 'col'),...]
    pallas_call x1, Pallas kernels: 229 us -> 255 us  [exchange(): pl.pallas_call(functools.partial(exchange_kernel, groups, cols, stride),...]
    unnamed x12 -> x5, local copies, waits for them, and re-layouts: 15.7 us -> 2.76 us
    all_to_all x2 -> x0, waiting for transfers between devices: 12.3 us -> none  [the longest x1 12.3 us: body(): lax.all_to_all(partial_value.reshape(1, full_width, -1), ('grp', 'col'),...]
    reduce_sum x1 -> x0, other arithmetic: 8.1 us -> none  [pool_rows(): return jnp.sum(picked * weights[None, :, :], axis=2)]
  transfers between devices with their start and end apart: 2 -> 0, of which waited for: 1 -> 0; matrix products, arithmetic and copies ran while one was open for 4% -> 0% of each run, Pallas kernels for 64% -> 0%
where the time goes in v2:
time: 281 us
  Pallas kernels  267 us (95%)
  local copies, waits for them, and re-layouts  9.09 us (3%)
  other arithmetic  3.94 us (1%)
    pallas_call x1, Pallas kernels, exchange(): pl.pallas_call(functools.partial(exchange_kernel, groups, cols, stride),...  255 us
    pallas_call x1, Pallas kernels, unpack(): pl.pallas_call(unpack_kernel, out_shape=jax.ShapeDtypeStruct((per_group,...  12.4 us

profile of v2, /device:TPU:4, one launch (start us, length us, event | category | flops | bytes accessed | tf_op | source)
XLA Modules:
  0.0 280.7 jit_solution(227072242279787710)
XLA Ops:
  0.6 0.0 copy-start
  0.6 0.8 select_reduce_fusion
  1.4 0.7 compare_select_fusion.3
  2.1 1.7 gather_fusion
  3.8 0.0 copy-done
  3.8 1.2 gather_fusion.1
  5.0 0.5 and_select_fusion.units_ref
  5.6 1.1 copy.16
  6.7 0.8 copy.15
  7.5 0.2 fusion
  7.7 0.7 compare_select_fusion.2
  8.3 0.8 gather_fusion.2
  9.1 0.7 compare_and_fusion.1
  9.8 0.2 broadcast_select_fusion
  10.0 0.2 copy.17
  10.2 0.8 copy.18.ids_ref
  10.9 254.6 %exchange.1 = (bf16[32,4,8,32,128]{4,3,2,1,0:T(8,128)(2,1)}, f32[128,8,128]{2,1,0:T(8,128)}) custom-call(s32[128]{0:T(128)} %gather_fusion, s32[128]{0:T(128)} %and_select_fusion.units_ref, s32[128,1,128]{2,1,0:T(1,128)} %copy.18.ids_ref, bf16[1,128,32768]{2,1,0:T(8,128)(2,1)} %table_ref.1), custom_call_target="tpu_custom_call" | custom-call | tf_op jit(solution)/shard_map/exchange/pallas_call | solution.py:195
  265.5 1.7 gather_fusion.3
  267.2 0.2 select_bitcast_fusion
  267.4 0.9 copy.19
  268.3 12.4 %unpack.1 = bf16[4,32,32768]{2,1,0:T(8,128)(2,1)} custom-call(bf16[32,4,8,32,128]{4,3,2,1,0:T(8,128)(2,1)} %get-tuple-element.4.in_ref), custom_call_target="tpu_custom_call" | custom-call | tf_op jit(solution)/shard_map/unpack/pallas_call | solution.py:235
  (5 shorter events, 0.0 us)
Async XLA Ops:
  0.6 3.2 %copy-start = (s32[128]{0:T(128)S(1)}, s32[128]{0:T(128)}, u32[]{:S(2)}) copy-start(s32[128]{0:T(128)} %param.7) | copy-start | bytes 1540

commit v3 on v2

--- a/solution.py
+++ b/solution.py
@@ -11,13 +11,7 @@
 LANES = 128
 UNIT = 4096
 BAG = 16
-
-
-def invert(permutation):
-    entries = permutation.shape[0]
-    across = lax.broadcasted_iota(jnp.int32, (entries, entries), 1)
-    down = lax.broadcasted_iota(jnp.int32, (entries, entries), 0)
-    return jnp.sum(jnp.where(permutation[None, :] == down, across, 0), axis=1)
+ROWS = 32768
 
 
 def place(index):
@@ -52,6 +46,15 @@
     own = grp * cols + col
     me = (lax.div(grp, 8), lax.rem(lax.div(grp, 2), 4), lax.rem(grp, 2), col)
 
+    barrier = pltpu.get_barrier_semaphore()
+
+    def greet(i, carry):
+        to_grp, to_col = peer_of(i, me)
+        pl.semaphore_signal(barrier, inc=1, device_id=(to_grp, to_col), device_id_type=MESH)
+        return carry
+
+    lax.fori_loop(1, devices, greet, 0)
+
     def load(j, carry):
         pltpu.make_async_copy(
             table_ref.at[0, :, pl.ds(pl.multiple_of(j * LANES, LANES), LANES)],
@@ -61,6 +64,7 @@
         return carry
 
     lax.fori_loop(0, column_blocks, load, 0)
+    pl.semaphore_wait(barrier, devices - 1)
 
     def send_ids(i, carry):
         to_grp, to_col = peer_of(lax.rem(i * stride, devices), me)
@@ -97,11 +101,14 @@
     table_len = column_blocks * LANES
 
     def turn(j, carry):
-        block = blocks[lax.div(j, groups), lax.rem(j, groups)].astype(jnp.float32)
-        rows_by_id[pl.ds(pl.multiple_of(j * LANES, LANES), LANES), :] = block.T
-        return carry
-
-    lax.fori_loop(0, column_blocks, turn, 0)
+        for u in range(4):
+            p = lax.rem(j, groups // 4) * 4 + u
+            unit = lax.div(j, groups // 4)
+            start = pl.multiple_of((unit * groups + p) * LANES, LANES)
+            rows_by_id[pl.ds(start, LANES), :] = blocks[unit, p].T.astype(jnp.float32)
+        return carry
+
+    lax.fori_loop(0, column_blocks // 4, turn, 0)
     rows_by_id[pl.ds(table_len, 8), :] = jnp.zeros((8, width), jnp.float32)
     others_ids = ids_in.at[pl.ds(0, devices - 1)]
     pltpu.make_async_copy(others_ids, others_ids, ids_recv_sem).wait()
@@ -155,11 +162,12 @@
     lax.fori_loop(0, groups * per_group, pack, 0)
 
     def send2(i, carry):
-        offset = lax.rem(i * 5, groups)
-        to_grp, _ = peer_of(offset, me)
+        offset = lax.rem(lax.rem(i, groups - 1) + 1, groups) * 27
+        q = lax.div(i, groups - 1)
+        to_grp, _ = peer_of(lax.rem(offset, groups), me)
         pltpu.make_async_remote_copy(
-            src_ref=packed.at[to_grp],
-            dst_ref=out_ref.at[grp],
+            src_ref=packed.at[to_grp, q],
+            dst_ref=out_ref.at[grp, q],
             send_sem=send2_sem,
             recv_sem=recv2_sem,
             device_id=(to_grp, col),
@@ -167,7 +175,7 @@
         ).start()
         return carry
 
-    lax.fori_loop(1, groups, send2, 0)
+    lax.fori_loop(0, per_group * (groups - 1), send2, 0)
     mine = pltpu.make_async_copy(packed.at[grp], out_ref.at[grp], local_sem)
     mine.start()
     mine.wait()
@@ -216,48 +224,110 @@
         ]
         + [pltpu.SemaphoreType.DMA] * 9,
         compiler_params=pltpu.CompilerParams(
-            has_side_effects=True, vmem_limit_bytes=60 * 1024 * 1024
+            collective_id=0, has_side_effects=True, vmem_limit_bytes=60 * 1024 * 1024
         ),
         name="exchange",
     )(slots, counts, ids, old_tables)
 
 
-def unpack_kernel(in_ref, out_ref):
+def plan_kernel(devices, old_ref, new_ref, rows_ref, ids_ref, len_ref, slots_ref, counts_ref, inv_ref, ids_out, turned):
+    def invert(s, carry):
+        inv_ref[old_ref[s]] = s
+        return carry
+
+    lax.fori_loop(0, devices, invert, 0)
+
+    def place_of(j, carry):
+        table = new_ref[j]
+        slots_ref[j] = inv_ref[table]
+        counts_ref[j] = lax.div(rows_ref[table], UNIT)
+        return carry
+
+    lax.fori_loop(0, devices, place_of, 0)
+    samples, tables = len_ref.shape
+    turn_in = lax.broadcasted_iota(jnp.int32, (BAG, tables), 0)
+    parts = []
+    for b in range(samples):
+        used = turn_in < len_ref[b : b + 1, :]
+        parts.append(jnp.where(used, ids_ref[b * BAG : (b + 1) * BAG, :], ROWS))
+    turned[...] = jnp.concatenate(parts, axis=0).T
+
+    def pick(s, carry):
+        for u in range(8):
+            ids_out[s * 8 + u] = turned[pl.ds(old_ref[s * 8 + u], 1), :]
+        return carry
+
+    lax.fori_loop(0, devices // 8, pick, 0)
+
+
+def plan(old_plan, new_plan, table_rows, ids, bag_len):
+    tables = old_plan.shape[0]
+    smem = pl.BlockSpec(memory_space=pltpu.SMEM)
+    vmem = pl.BlockSpec(memory_space=pltpu.VMEM)
+    small = jax.ShapeDtypeStruct((tables,), jnp.int32)
+    flat = jnp.transpose(ids, (0, 2, 1)).reshape(-1, tables)
+    return pl.pallas_call(
+        functools.partial(plan_kernel, tables),
+        out_shape=(small, small, small, jax.ShapeDtypeStruct((tables, 1, flat.shape[0]), jnp.int32)),
+        in_specs=[smem, smem, smem, vmem, vmem],
+        out_specs=(smem, smem, smem, vmem),
+        scratch_shapes=[pltpu.VMEM((tables, flat.shape[0]), jnp.int32)],
+        name="plan",
+    )(old_plan, new_plan, table_rows, flat, bag_len)
+
+
+def unpack_kernel(step, inv_ref, in_ref, ret_ref, out_ref, pooled_ref):
     groups, _, units = in_ref.shape[:3]
     for k in range(units):
         for p in range(groups):
             start = (k * groups + p) * LANES
             out_ref[0, :, start : start + LANES] = in_ref[p, 0, k]
-
-
-def unpack(received, step=2):
+    tables = inv_ref.shape[0]
+    samples = pooled_ref.shape[0]
+    share = tables // step
+    first = (pl.program_id(0) * pl.num_programs(1) + pl.program_id(1)) * share
+
+    def reorder(i, carry):
+        table = first + i
+        rows = ret_ref[inv_ref[table]]
+        for b in range(samples):
+            pooled_ref[b, pl.ds(table, 1), :] = rows[b : b + 1, :]
+        return carry
+
+    lax.fori_loop(0, share, reorder, 0)
+
+
+def unpack(inverse, received, returned, step=4):
     groups, per_group, units, narrow, lanes = received.shape
+    devices, samples, width = returned.shape
+    grid = (per_group, units // step)
     return pl.pallas_call(
-        unpack_kernel,
-        out_shape=jax.ShapeDtypeStruct((per_group, narrow, units * groups * lanes), received.dtype),
-        grid=(per_group, units // step),
-        in_specs=[pl.BlockSpec((groups, 1, step, narrow, lanes), lambda q, k: (0, q, k, 0, 0))],
-        out_specs=pl.BlockSpec((1, narrow, step * groups * lanes), lambda q, k: (q, 0, k)),
+        functools.partial(unpack_kernel, per_group * units // step),
+        out_shape=(
+            jax.ShapeDtypeStruct((per_group, narrow, units * groups * lanes), received.dtype),
+            jax.ShapeDtypeStruct((samples, devices, width), returned.dtype),
+        ),
+        grid=grid,
+        in_specs=[
+            pl.BlockSpec(memory_space=pltpu.SMEM),
+            pl.BlockSpec((groups, 1, step, narrow, lanes), lambda q, k: (0, q, k, 0, 0)),
+            pl.BlockSpec((devices, samples, width), lambda q, k: (0, 0, 0)),
+        ],
+        out_specs=(
+            pl.BlockSpec((1, narrow, step * groups * lanes), lambda q, k: (q, 0, k)),
+            pl.BlockSpec((samples, devices, width), lambda q, k: (0, 0, 0)),
+        ),
+        compiler_params=pltpu.CompilerParams(vmem_limit_bytes=40 * 1024 * 1024),
         name="unpack",
-    )(received)
+    )(inverse, received, returned)
 
 
 def body(old_tables, table_rows, old_plan, new_plan, ids, bag_len):
     group_count = lax.axis_size("grp")
     col_count = lax.axis_size("col")
-    bag_size = ids.shape[2]
-    old_inverse = invert(old_plan)
-    slots = old_inverse[new_plan]
-    counts = table_rows[new_plan] // UNIT
-    bag_iota = lax.broadcasted_iota(jnp.int32, (1, 1, bag_size), 2)
-    marked = jnp.where(bag_iota < bag_len[:, :, None], ids, old_tables.shape[2])
-    by_slot = jnp.take(marked, old_plan, axis=1)
-    own_ids = jnp.transpose(by_slot, (1, 0, 2)).reshape(-1, 1, LANES)
+    slots, counts, inverse, own_ids = plan(old_plan, new_plan, table_rows, ids, bag_len)
     received, returned = exchange(slots, counts, own_ids, old_tables, group_count, col_count)
-    new_local = unpack(received)
-    by_table = jnp.take(returned, old_inverse, axis=0)
-    pooled = jnp.transpose(by_table, (1, 0, 2))
-    return (new_local, pooled)
+    return unpack(inverse, received, returned)
 
 
 def solution(mesh):

time: 281 us -> 242 us (0.86)
  Pallas kernels: 267 us -> 236 us
  local copies, waits for them, and re-layouts: 9.09 us -> 4.42 us
  other arithmetic: 3.94 us -> 0 us
    pallas_call x1, Pallas kernels: 255 us -> 225 us  [exchange(): pl.pallas_call(functools.partial(exchange_kernel, groups, cols, stride),...]
    gather x4 -> x0, local copies, waits for them, and re-layouts: 5.39 us -> none  [the longest x1 1.72 us: body(): slots = old_inverse[new_plan]]
    pallas_call x1 -> x2, Pallas kernels: 12.4 us -> 10.7 us  [the longest x1 6.43 us: unpack(): pl.pallas_call(functools.partial(unpack_kernel, per_group * units // step...]
where the time goes in v3:
time: 242 us; the launch traced here: 241 us
  Pallas kernels  236 us (98%)
  local copies, waits for them, and re-layouts  4.42 us (2%)
    pallas_call x1, Pallas kernels, exchange(): pl.pallas_call(functools.partial(exchange_kernel, groups, cols, stride),...  225 us
    pallas_call x1, Pallas kernels, unpack(): pl.pallas_call(functools.partial(unpack_kernel, per_group * units // step...  6.43 us

profile of v3, /device:TPU:4, one launch (start us, length us, event | category | flops | bytes accessed | tf_op | source)
XLA Modules:
  0.0 240.8 jit_solution(2035852729465145844)
XLA Ops:
  0.6 4.3 %plan.1 = (s32[128]{0:T(128)}, s32[128]{0:T(128)}, s32[128]{0:T(128)}, s32[128,1,128]{2,1,0:T(1,128)}) custom-call(s32[128]{0:T(128)} %old_ref.1, s32[128]{0:T(128)} %new_ref.1, s32[128]{0:T(128)} %rows_ref.1, s32[128,128]{1,0:T(8,128)} %bitcast.3, s32[8,128]{1,0:T(8,128)} %len_ref.1), custom_call_target="tpu_custom_call" | custom-call | tf_op jit(solution)/shard_map/plan/pallas_call | solution.py:269
  4.9 0.0 copy-start.2
  5.0 225.0 %exchange.1 = (bf16[32,4,8,32,128]{4,3,2,1,0:T(8,128)(2,1)}, f32[128,8,128]{2,1,0:T(8,128)}) custom-call(s32[128]{0:T(128)} %get-tuple-element.9.slots_ref, s32[128]{0:T(128)} %get-tuple-element.10.units_ref, s32[128,1,128]{2,1,0:T(1,128)} %get-tuple-element.11.ids_ref, bf16[1,128,32768]{2,1,0:T(8,128)(2,1)} %table_ref.1), custom_call_target="tpu_custom_call" | custom-call | tf_op jit(solution)/shard_map/exchange/pallas_call | solution.py:203
  229.9 0.0 copy-done.2
  229.9 0.0 copy-start
  229.9 3.4 %copy-done = bf16[32,4,8,32,128]{4,3,2,1,0:T(8,128)(2,1)S(1)} copy-done((bf16[32,4,8,32,128]{4,3,2,1,0:T(8,128)(2,1)S(1)}, bf16[32,4,8,32,128]{4,3,2,1,0:T(8,128)(2,1)}, u32[]{:S(2)}) %copy-start) | copy-done | bytes 8388632
  233.3 0.0 copy-start.1
  233.3 1.0 copy-done.1
  234.4 6.4 %unpack.1 = (bf16[4,32,32768]{2,1,0:T(8,128)(2,1)}, f32[8,128,128]{2,1,0:T(8,128)}) custom-call(s32[128]{0:T(128)S(1)} %copy-done.2, bf16[32,4,8,32,128]{4,3,2,1,0:T(8,128)(2,1)S(1)} %copy-done, f32[128,8,128]{2,1,0:T(8,128)S(1)} %copy-done.1), custom_call_target="tpu_custom_call" | custom-call | tf_op jit(solution)/shard_map/unpack/pallas_call | solution.py:304
Async XLA Ops:
  4.9 225.0 %copy-start.2 = (s32[128]{0:T(128)S(1)}, s32[128]{0:T(128)}, u32[]{:S(2)}) copy-start(s32[128]{0:T(128)} %get-tuple-element.8.inv_ref) | copy-start | bytes 1540
  229.9 3.4 %copy-start = (bf16[32,4,8,32,128]{4,3,2,1,0:T(8,128)(2,1)S(1)}, bf16[32,4,8,32,128]{4,3,2,1,0:T(8,128)(2,1)}, u32[]{:S(2)}) copy-start(bf16[32,4,8,32,128]{4,3,2,1,0:T(8,128)(2,1)} %get-tuple-element.12.in_ref) | copy-start | bytes 25165828
  233.3 1.0 copy-start.1
